TPU v7x, 256 devices: a whole 4x4x8 slice. The times are simulated.
256 devices in a mesh: row: 16 (over z, x_lo), col: 8 (over y, x_hi), depth: 2 (over core).
Axes of the slice: x: 4 (x_hi: 2, x_lo: 2; x = x_hi * 2 + x_lo), y: 4, z: 8, core: 2. Of those that a mesh axis runs over, the one named last changes fastest.
Arguments:
- matrix: float32 [2, 16, 512, 4, 8, 512], P(None, 'row', None, None, 'col'), may hold values from 0 to 5
Outputs:
- factored: float32 [2, 16, 512, 4, 8, 512], P(None, 'row', 'depth', None, 'col')
All inputs are finite; a program needn't handle non-finite values.
Results may differ from a plain program's by a relative error of at most 0.00021.
Values sent between devices are 32-bit elements; how exact they have to be, the bound alone decides.
A program may use at most 128 MiB of HBM per device.

v0:
```python
import jax
import jax.numpy as jnp
from jax import lax
from jax.sharding import Mesh
from jax.sharding import PartitionSpec as P

STEPS = 2
ROW = ("row_0", "row_1")


def split_up(x, dim, size):
    before, after = (x.shape[:dim], x.shape[dim + 1 :])
    return jnp.moveaxis(x.reshape(*before, size, -1, *after), dim, 0)


def summed_on_arrival(x, axis, dim):
    blocks = split_up(x, dim, lax.axis_size(axis))
    arrived = lax.all_to_all(blocks, axis, split_axis=0, concat_axis=0, tiled=True)
    return arrived.sum(axis=0)


def spread(x, axes, root):
    x = jnp.where(lax.axis_index(axes) == root, x, jnp.zeros_like(x))
    for axis in axes:
        x = lax.psum(x, axis)
    return x


def from_everyone(x, axis):
    size = lax.axis_size(axis)
    return lax.all_to_all(jnp.broadcast_to(x[None], (size, *x.shape)), axis, 0, 0, tiled=True)


def laid_out(blocks, dim):
    shape = list(blocks.shape[1:])
    shape[dim] *= blocks.shape[0]
    return jnp.moveaxis(blocks, 0, dim).reshape(shape)


def gathered_copies(x, axis, dim):
    blocks = from_everyone(x, axis)
    return laid_out(blocks, dim)


def broadcast(x, axis, root):
    return lax.dynamic_index_in_dim(lax.all_gather(x, axis), root, 0, keepdims=False)


def body(matrix):
    tiles_rows = matrix.shape[0]
    tile = matrix.shape[2]
    tiles_cols = matrix.shape[3]
    grid_rows = lax.axis_size(ROW)
    grid_cols = lax.axis_size("col")
    layers_count = lax.axis_size("depth")
    half_width = tile // layers_count
    depth_index = lax.axis_index("depth")
    row_index = lax.axis_index(ROW)
    col_index = lax.axis_index("col")
    local = matrix.reshape(tiles_rows, tile, tiles_cols, tile)
    keeper = (depth_index == 0).astype(jnp.float32)
    columns = [local[:, :, j, :] * keeper for j in range(tiles_cols)]
    global_rows = jnp.arange(tiles_rows, dtype=jnp.int32) * grid_rows + row_index
    global_cols = jnp.arange(tiles_cols, dtype=jnp.int32) * grid_cols + col_index
    identity = jnp.eye(tile, dtype=jnp.float32)
    stored = []
    for section in range(STEPS):
        owner_col = section % grid_cols
        slot_col = section // grid_cols
        reduced = summed_on_arrival(columns[slot_col], "depth", 1)
        shared = broadcast(reduced, "col", owner_col)
        owner_row = section % grid_rows
        slot_row = section // grid_rows
        halves = spread(shared[slot_row], ROW, owner_row)
        diag = gathered_copies(halves, "depth", 0)
        diag_factor = jnp.linalg.cholesky(diag)
        inverse_factor = jax.scipy.linalg.solve_triangular(diag_factor, identity, lower=True)
        solved = jnp.einsum(
            "ipb,cb->ipc",
            shared,
            inverse_factor,
            precision=lax.Precision.HIGHEST,
            preferred_element_type=jnp.float32,
        )
        own_rows = lax.dynamic_slice_in_dim(diag_factor, depth_index * half_width, half_width, 0)
        below = (global_rows > section)[:, None, None]
        at_diag = (global_rows == section)[:, None, None]
        panel = jnp.where(below, solved, jnp.where(at_diag, own_rows[None], 0.0))
        rows_half = lax.all_to_all(panel, "depth", split_axis=2, concat_axis=1, tiled=True)
        stored.append(panel)
        rows_half = rows_half * (global_rows > section).astype(jnp.float32)[:, None, None]
        tiles_out = []
        for crossing_j in range(tiles_cols):
            target = global_cols[crossing_j]
            owner = target % grid_rows
            slot = target // grid_rows
            piece = lax.dynamic_index_in_dim(rows_half, slot, 0, keepdims=False)
            tiles_out.append(spread(piece, ROW, owner))
        for j in range(tiles_cols):
            columns[j] = columns[j] - jnp.einsum(
                "ipe,qe->ipq",
                rows_half,
                tiles_out[j],
                precision=lax.Precision.HIGHEST,
                preferred_element_type=jnp.float32,
            )
    whole = jnp.stack(columns, axis=2)
    summed = summed_on_arrival(whole, "depth", 1)
    upper = (global_rows < STEPS)[:, None, None, None] & (global_cols >= STEPS)[None, None, :, None]
    summed = jnp.where(upper, 0.0, summed)
    for section in range(STEPS):
        owner_col = section % grid_cols
        slot_col = section // grid_cols
        hit = col_index == owner_col
        summed = summed.at[:, :, slot_col, :].set(
            jnp.where(hit, stored[section], summed[:, :, slot_col, :])
        )
    return summed.reshape(tiles_rows, 1, half_width, tiles_cols, 1, tile)


def solution(mesh):
    split = Mesh(
        mesh.devices.reshape(8, 2, mesh.shape["col"], mesh.shape["depth"]),
        ("row_0", "row_1", "col", "depth"),
    )
    placed = (P(None, ROW, None, None, "col", None),)
    return jax.shard_map(
        body,
        mesh=split,
        in_specs=placed,
        out_specs=P(None, ROW, "depth", None, "col", None),
        check_vma=False,
    )
```

profile of v0, /device:TPU:38, one launch (start us, length us, event | category | flops | bytes accessed | tf_op | source)
XLA Modules:
  0.0 1219.7 jit_solution(510988850766627012)
XLA Ops:
  28.4 112.7 %all-gather.5.cloned.1.call-done = f32[16,256,512]{2,1,0:T(8,128)} async-done(((f32[2,256,512]{2,1,0:T(8,128)}), f32[16,256,512]{2,1,0:T(8,128)}) %all-gather.5.cloned.1.call-update) | async-done | bytes 8388624 | tf_op jit(solution)/shard_map/all_gather | solution.py:46
  143.0 73.4 %all-reduce.12.cloned.1.call-done = f32[256,512]{1,0:T(8,128)} async-done(((f32[256,512]{1,0:T(8,128)}), f32[256,512]{1,0:T(8,128)}) %all-reduce.12.cloned.1.call-update) | async-done | bytes 524304 | tf_op jit(solution)/shard_map/psum | solution.py:25
  228.8 28.5 %all-reduce.14.cloned.1.call-done = f32[256,512]{1,0:T(8,128)} async-done(((f32[256,512]{1,0:T(8,128)}), f32[256,512]{1,0:T(8,128)}) %all-reduce.14.cloned.1.call-update) | async-done | bytes 524304 | tf_op jit(solution)/shard_map/psum | solution.py:25
  267.1 11.7 cholesky.286
  278.9 9.8 custom-call.27
  291.3 11.7 cholesky.305
  303.1 10.0 custom-call.28
  314.7 11.7 cholesky.326
  327.1 9.8 custom-call.29
  338.4 11.7 cholesky.343
  357.4 11.0 while.6
  369.2 40.1 %custom-call.30 = f32[4,128,128]{1,2,0:T(8,128)S(1)} custom-call(f32[4,128,128]{2,1,0:T(8,128)} %copy-done.18), custom_call_target="InvertDiagBlocksLowerTriangular" | custom-call | tf_op jit(solution)/shard_map/jit(_solve_triangular)/triangular_solve | solution.py:77
  419.6 6.6 all_to_all.62
  431.3 75.2 %all-reduce.16.cloned.1.call-done = f32[512,256]{1,0:T(8,128)} async-done(((f32[512,256]{1,0:T(8,128)}), f32[512,256]{1,0:T(8,128)}) %all-reduce.16.cloned.1.call-update) | async-done | bytes 524304 | tf_op jit(solution)/shard_map/psum | solution.py:25
  506.6 40.7 %all-reduce.18.cloned.1.call-done = f32[512,256]{1,0:T(8,128)} async-done(((f32[512,256]{1,0:T(8,128)}), f32[512,256]{1,0:T(8,128)}) %all-reduce.18.cloned.1.call-update) | async-done | bytes 524304 | tf_op jit(solution)/shard_map/psum | solution.py:25
  558.4 111.8 %all-gather.7.cloned.1.call-done = f32[16,256,512]{2,1,0:T(8,128)} async-done(((f32[2,256,512]{2,1,0:T(8,128)}), f32[16,256,512]{2,1,0:T(8,128)}) %all-gather.7.cloned.1.call-update) | async-done | bytes 8388624 | tf_op jit(solution)/shard_map/all_gather | solution.py:46
  672.1 73.4 %all-reduce.20.cloned.1.call-done = f32[256,512]{1,0:T(8,128)} async-done(((f32[256,512]{1,0:T(8,128)}), f32[256,512]{1,0:T(8,128)}) %all-reduce.20.cloned.1.call-update) | async-done | bytes 524304 | tf_op jit(solution)/shard_map/psum | solution.py:25
  745.6 40.8 %all-reduce.22.cloned.1.call-done = f32[256,512]{1,0:T(8,128)} async-done(((f32[256,512]{1,0:T(8,128)}), f32[256,512]{1,0:T(8,128)}) %all-reduce.22.cloned.1.call-update) | async-done | bytes 524304 | tf_op jit(solution)/shard_map/psum | solution.py:25
  794.0 11.7 cholesky.358
  805.9 9.8 custom-call.31
  818.2 11.7 cholesky.377
  831.2 10.0 custom-call.32
  842.8 11.7 cholesky.398
  855.3 9.8 custom-call.33
  866.5 11.7 cholesky.415
  883.5 11.3 while.7
  894.8 39.3 %custom-call.34 = f32[4,128,128]{1,2,0:T(8,128)S(1)} custom-call(f32[4,128,128]{2,1,0:T(8,128)S(1)} %get-tuple-element.46), custom_call_target="InvertDiagBlocksLowerTriangular" | custom-call | tf_op jit(solution)/shard_map/jit(_solve_triangular)/triangular_solve | solution.py:77
  954.6 99.9 %all-reduce.24.cloned.1.call-done = (f32[512,256]{1,0:T(8,128)}, f32[512,256]{1,0:T(8,128)}, f32[512,256]{1,0:T(8,128)}, f32[512,256]{1,0:T(8,128)}, f32[512,256...) async-done(((f32[512,256]{1,0:T(8,128)}, f32[512,256]{1,0:T(8,128)}, f32[512,256]{1,0:T(8,128)}, f32[512,256]{1,0:T(8,128)}, f32[512,256]{1,0:T(8,128)}, ...) | async-done | bytes 3670032 | tf_op jit(solution)/shard_map/psum | solution.py:25
  1054.7 111.4 %all-reduce.26.cloned.1.call-done = (f32[512,256]{1,0:T(8,128)}, f32[512,256]{1,0:T(8,128)}, f32[512,256]{1,0:T(8,128)}, f32[512,256]{1,0:T(8,128)}, f32[512,256...) async-done(((f32[512,256]{1,0:T(8,128)}, f32[512,256]{1,0:T(8,128)}, f32[512,256]{1,0:T(8,128)}, f32[512,256]{1,0:T(8,128)}, f32[512,256]{1,0:T(8,128)}, ...) | async-done | bytes 3670032 | tf_op jit(solution)/shard_map/psum | solution.py:25
  1183.3 11.8 all_to_all.66
  1195.1 6.9 reduce_sum.31
  1206.3 6.3 copy.31
  (200 shorter events, 157.7 us)
Async XLA Ops:
  12.6 3.2 copy-start
  17.6 7.9 all-to-all-start
  22.5 118.6 %all-gather.5.cloned.1.call-start = ((), (), s32[]{:S(2)}) async-start(), calls=%async_computation.13 | async-start | bytes 9437184 | tf_op jit(solution)/shard_map/all_gather | solution.py:46
  28.3 188.1 %all-reduce.12.cloned.1.call-start = ((), (), s32[]{:S(2)}) async-start(), calls=%async_computation.7 | async-start | bytes 1048576 | tf_op jit(solution)/shard_map/psum | solution.py:25
  143.0 114.3 %all-reduce.14.cloned.1.call-start = ((), (), s32[]{:S(2)}) async-start(), calls=%async_computation.8 | async-start | bytes 1048576 | tf_op jit(solution)/shard_map/psum | solution.py:25
  216.4 290.1 %all-reduce.16.cloned.1.call-start = ((), (), s32[]{:S(2)}) async-start(), calls=%async_computation.9 | async-start | bytes 1048576 | tf_op jit(solution)/shard_map/psum | solution.py:25
  266.1 1.0 copy-start.9
  350.1 4.0 copy-start.7
  354.1 55.2 %copy-start.5 = (f32[512,512]{1,0:T(8,128)S(1)}, f32[512,512]{1,0:T(8,128)}, u32[]{:S(2)}) copy-start(f32[512,512]{1,0:T(8,128)} %fusion.28) | copy-start | bytes 3145732
  368.4 0.7 copy-start.18
  411.0 4.2 copy-start.11
  418.3 7.9 copy-start.3
  431.3 116.0 %all-reduce.18.cloned.1.call-start = ((), (), s32[]{:S(2)}) async-start(), calls=%async_computation.10 | async-start | bytes 1048576 | tf_op jit(solution)/shard_map/psum | solution.py:25
  506.6 163.6 %all-gather.7.cloned.1.call-start = ((), (), s32[]{:S(2)}) async-start(), calls=%async_computation.14 | async-start | bytes 9437184 | tf_op jit(solution)/shard_map/all_gather | solution.py:46
  550.3 1.3 copy-start.2
  558.3 187.1 %all-reduce.20.cloned.1.call-start = ((), (), s32[]{:S(2)}) async-start(), calls=%async_computation.11 | async-start | bytes 1048576 | tf_op jit(solution)/shard_map/psum | solution.py:25
  672.1 114.3 %all-reduce.22.cloned.1.call-start = ((), (), s32[]{:S(2)}) async-start(), calls=%async_computation.12 | async-start | bytes 1048576 | tf_op jit(solution)/shard_map/psum | solution.py:25
  745.5 309.1 %all-reduce.24.cloned.1.call-start = ((), (), s32[]{:S(2)}) async-start(), calls=%async_computation.15 | async-start | bytes 7340032 | tf_op jit(solution)/shard_map/psum | solution.py:25
  793.0 1.0 copy-start.8
  881.5 52.7 %copy-start.6 = (f32[512,512]{1,0:T(8,128)S(1)}, f32[512,512]{1,0:T(8,128)}, u32[]{:S(2)}) copy-start(f32[512,512]{1,0:T(8,128)} %fusion.28) | copy-start | bytes 3145732
  935.8 4.2 copy-start.10
  954.4 211.7 %all-reduce.26.cloned.1.call-start = ((), (), s32[]{:S(2)}) async-start(), calls=%async_computation.16 | async-start | bytes 7340032 | tf_op jit(solution)/shard_map/psum | solution.py:25
  1166.1 3.8 copy-start.17
  1166.1 9.4 slice-start
  1169.9 1.9 copy-start.16
  1169.9 5.7 slice-start.1
  1171.8 1.9 copy-start.15
  1173.6 1.9 copy-start.14
  1175.6 2.2 copy-start.13
  1177.7 2.2 copy-start.12
  1201.9 3.4 copy-start.1
  1201.9 3.7 copy-start.4
Sparse Core Ops, SparseCore 0:
  28.5 112.5 all-gather.4
  143.4 72.9 all-reduce.11
  219.0 38.2 all-reduce.13
  431.4 75.1 all-reduce.15
  509.0 38.2 all-reduce.17
  558.4 111.6 all-gather.6
  672.5 72.9 all-reduce.19
  748.1 38.2 all-reduce.21
  954.5 99.9 all-reduce.23
  1057.5 108.5 all-reduce.25
where the time goes:
time: 1230 us; the launch traced here: 1220 us
  waiting for transfers between devices  771 us (63%)
  other arithmetic  271 us (22%)
  local copies, waits for them, and re-layouts  56.1 us (5%)
  matrix products  47.6 us (4%)
  blocking collectives  38.6 us (3%)
  between operations  30.2 us (2%)
    psum x8, waiting for transfers between devices, spread(): x = lax.psum(x, axis)  543 us
    all_gather x2, waiting for transfers between devices, broadcast(): lax.all_gather(x, axis)  224 us
    another operation x29, other arithmetic, body(): diag_factor = jnp.linalg.cholesky(diag)  158 us
    another operation x5, other arithmetic, body(): jax.scipy.linalg.solve_triangular(diag_factor, identity, lower=True)  84.6 us
  transfers between devices with their start and end apart: 11, of which 11 were waited for; matrix products, arithmetic and copies ran while one was open for 0% of the time, Pallas kernels for 0%

commit v1 on v0

v1 whole, which is shorter than its diff:
```python
import functools

import jax
import jax.numpy as jnp
from jax import lax
from jax.experimental import pallas as pl
from jax.experimental.pallas import tpu as pltpu
from jax.sharding import PartitionSpec as P

T = 512
B = 128
NB = 2 * T // B
RN = 32
RR = T // RN
CR = 64
HI = lax.Precision.HIGHEST
MESH = pl.DeviceIdType.MESH
F32 = jnp.float32
BF16 = jnp.bfloat16


def mm(a, b, dims=((1,), (0,)), precision=None):
    return lax.dot_general(a, b, (dims, ((), ())), precision=precision, preferred_element_type=F32)


def split(x):
    h = x.astype(BF16)
    return h, (x - h.astype(F32)).astype(BF16)


def mm3(a, b, dims=((1,), (0,))):
    return mm(a[0], b[0], dims) + (mm(a[0], b[1], dims) + mm(a[1], b[0], dims))


def base(a, w):
    out = []
    sub = lax.broadcasted_iota(jnp.int32, (8, B), 0)
    lane = lambda x, k: jnp.broadcast_to(x[:, k : k + 1], (8, B))
    row = lambda x, m: jnp.broadcast_to(x[m : m + 1, :], (8, B))
    for g in range(16):
        cg = [lane(a[g], 8 * g + n) for n in range(8)]
        e = [[row(cg[n], m) if n >= m else None for n in range(8)] for m in range(8)]
        ar = [row(a[g], m) for m in range(8)]
        wr = [row(w[g], m) for m in range(8)]
        rs = [None] * 8
        u = [[None] * 8 for _ in range(8)]
        for m in range(8):
            rs[m] = lax.rsqrt(e[m][m])
            for n in range(m + 1, 8):
                u[m][n] = e[m][n] * rs[m]
            ar[m] = ar[m] * rs[m]
            wr[m] = wr[m] * rs[m]
            for m2 in range(m + 1, 8):
                for n in range(m2, 8):
                    e[m2][n] = e[m2][n] - u[m][m2] * u[m][n]
                ar[m2] = ar[m2] - u[m][m2] * ar[m]
                wr[m2] = wr[m2] - u[m][m2] * wr[m]
        o = wr[0]
        for m in range(1, 8):
            o = jnp.where(sub == m, wr[m], o)
        out.append(o)
        for h in range(g + 1, 16):
            c = [lane(a[h], 8 * g + n) for n in range(8)]
            for m in range(8):
                f = c[m] * rs[m]
                for n in range(m + 1, 8):
                    c[n] = c[n] - f * u[m][n]
                a[h] = a[h] - f * ar[m]
                w[h] = w[h] - f * wr[m]
    return out


def kernel(
    x, out, rbuf, cbuf, fbuf, dbuf, abuf, vh, vl, lh, ll, wbuf, sbuf,
    r_rec, c_rec, f_rec, d_rec, rz_s, rx_s, rs_s, cy_s, cx_s, cs_s, f_s, d_s, loc,
):
    p, q, d = lax.axis_index("row"), lax.axis_index("col"), lax.axis_index("depth")
    z, xl = p // 2, p % 2
    y, xh = q // 2, q % 2
    xx = xh * 2 + xl
    dev = lambda zz, xli, yy, xhi, dd: (zz * 2 + xli, yy * 2 + xhi, dd)
    sib = dev(z, xl, y, xh, 1 - d)
    both = jnp.logical_and

    def remote(src, dst, ssem, rsem, to):
        return pltpu.make_async_remote_copy(
            src_ref=src, dst_ref=dst, send_sem=ssem, recv_sem=rsem, device_id=to, device_id_type=MESH
        )

    def arrived(dst, rsem):
        pltpu.make_async_copy(dst, dst, rsem).wait()

    def when_start(cond, copy, op):
        @pl.when(cond)
        def _():
            c = copy()
            c.start() if op else c.wait_send()

    rpiece = lambda k, n: rbuf.at[pl.ds(pl.multiple_of(k * T + n * RR, 8), RR), :]
    xr = lambda n: x.at[pl.ds(pl.multiple_of(n * RR, 8), RR), :]

    def cpiece(k, h, s, r):
        return cbuf.at[
            pl.ds(pl.multiple_of(h * T + s * 256 + r * CR, 8), CR), pl.ds(pl.multiple_of(k * T, B), T)
        ]

    xc = lambda h, s, r: x.at[pl.ds(pl.multiple_of(s * T + h * 256 + r * CR, 8), CR), pl.ds(0, T)]
    fpiece = lambda b, c: fbuf.at[pl.ds(pl.multiple_of(b * B, B), B), pl.ds(pl.multiple_of(c * B, B), B)]

    def r_own(n, src, op):
        up = n % 2 == 0
        nxt = jnp.where(up, (z + 1) % 8, (z + 7) % 8)
        more = jnp.where(up, z != 7, z != 1)
        when_start(
            more, lambda: remote(src, rpiece(xl, n), rz_s.at[n], r_rec.at[xl, n], dev(nxt, xl, y, xh, 0)), op
        )
        when_start(
            z >= 0, lambda: remote(src, rpiece(xl, n), rx_s.at[n], r_rec.at[xl, n], dev(z, 1 - xl, y, xh, 0)), op
        )

    def r_sib(k, n, op):
        when_start(
            z >= 0, lambda: remote(rpiece(k, n), rpiece(k, n), rs_s.at[k, n], r_rec.at[k, n], sib), op
        )

    def c_next(k, h, s, r, src, op):
        i = (k * 2 + s) * 4 + r
        nxt = jnp.where(h == 0, (y + 1) % 4, (y + 3) % 4)
        more = jnp.where(h == 0, y != 3, y != 1)
        when_start(
            more, lambda: remote(src, cpiece(k, h, s, r), cy_s.at[h, i], c_rec.at[h, i], dev(z, xl, nxt, xh, 0)), op
        )

    def c_cross(k, h, s, r, src, op):
        i = (k * 2 + s) * 4 + r
        when_start(
            z >= 0,
            lambda: remote(src, cpiece(k, h, s, r), cx_s.at[h, i], c_rec.at[h, i], dev(z, xl, y, 1 - xh, 0)), op,
        )

    def c_sib(k, h, s, r, op):
        i = (k * 2 + s) * 4 + r
        when_start(
            h == 1,
            lambda: remote(cpiece(k, h, s, r), cpiece(k, h, s, r), cs_s.at[i], c_rec.at[h, i], sib), op,
        )

    def f_send(b, c, op):
        v = fpiece(b, c)
        i = b * NB + c
        go = lambda cond, slot, to: when_start(
            cond, lambda: remote(v, v, f_s.at[slot, i], f_rec.at[i], to), op
        )
        root_line = both(z == 0, y == 0)
        go(both(root_line, xx == 0), 0, dev(z, 1, y, 0, 1))
        go(both(root_line, xx == 0), 1, dev(z, 1, y, 1, 1))
        go(both(root_line, xx == 1), 1, dev(z, 0, y, 1, 1))
        plane = y == 0
        go(both(plane, z <= 3), 2, dev((z + 1) % 8, xl, y, xh, 1))
        go(both(plane, (z == 0) | (z >= 6)), 3, dev((z + 7) % 8, xl, y, xh, 1))
        go((y == 0) | (y == 1), 4, dev(z, xl, (y + 1) % 4, xh, 1))
        go(y == 0, 5, dev(z, xl, (y + 3) % 4, xh, 1))
        go(z >= 0, 6, sib)

    def loop(n, f):
        lax.fori_loop(0, n, lambda i, s: (f(i), s)[1], 0)

    is_root = both(both(p == 0, q == 0), d == 1)
    src_r = z == 0
    src_c = y == 0

    own = [
        pltpu.make_async_copy(
            x.at[pl.ds(pl.multiple_of(s * T + d * 256, 8), 256), :], abuf.at[pl.ds(s * 256, 256), :], loc.at[s]
        )
        for s in range(2)
    ]
    for c in own:
        c.start()
    r_loc = pltpu.make_async_copy(
        x.at[pl.ds(0, T), :], rbuf.at[pl.ds(pl.multiple_of(xl * T, 8), T), :], loc.at[2]
    )
    c_loc = [
        pltpu.make_async_copy(
            x.at[pl.ds(pl.multiple_of(s * T + d * 256, 8), 256), pl.ds(0, T)],
            cbuf.at[pl.ds(pl.multiple_of(d * T + s * 256, 8), 256), pl.ds(pl.multiple_of(xh * T, B), T)],
            loc.at[3 + s],
        )
        for s in range(2)
    ]
    d_loc = pltpu.make_async_copy(x.at[pl.ds(0, T), pl.ds(0, T)], dbuf.at[pl.ds(0, T), pl.ds(0, T)], loc.at[5])

    @pl.when(src_r)
    def _():
        r_loc.start()

    @pl.when(src_c)
    def _():
        for c in c_loc:
            c.start()

    def d_copies(op):
        for i in range(4):
            when_start(
                both(both(p == 0, q == 1), d == 1),
                lambda: remote(
                    x.at[pl.ds(i * B, B), pl.ds(0, T)], dbuf.at[pl.ds(i * B, B), pl.ds(T, T)],
                    d_s.at[i], d_rec.at[i], (0, 0, 1),
                ),
                op,
            )
        when_start(
            both(both(p == 1, q == 1), d == 1),
            lambda: remote(
                x.at[pl.ds(0, T), pl.ds(0, T)], dbuf.at[pl.ds(T, T), pl.ds(T, T)], d_s.at[4], d_rec.at[4], (0, 0, 1)
            ),
            op,
        )

    d_copies(True)

    def source_copies(op):
        @pl.when(both(src_r, d == 0))
        def _():
            loop(RN, lambda n: r_own(n, xr(n), op))

        @pl.when(both(src_c, d == 0))
        def _():
            def one(i):
                for h in range(2):
                    c_next(xh, h, i // 4, i % 4, xc(h, i // 4, i % 4), op)
                    c_cross(xh, h, i // 4, i % 4, xc(h, i // 4, i % 4), op)

            loop(8, one)

    def forward(op):
        def step(t):
            for up in range(2):
                hops = z if up == 0 else 8 - z
                e = t - 2 * hops
                n = 2 * e + up

                @pl.when(both(both(e >= 0, e < RN // 2), z != 0))
                def _():
                    if op:
                        arrived(rpiece(xl, n), r_rec.at[xl, n])
                    r_own(n, rpiece(xl, n), op)
                    r_sib(xl, n, op)

                e2 = t - 2 * jnp.where(z == 0, 0, hops) - 2
                n2 = 2 * e2 + up

                @pl.when(both(e2 >= 0, e2 < RN // 2))
                def _():
                    if op:
                        arrived(rpiece(1 - xl, n2), r_rec.at[1 - xl, n2])
                    r_sib(1 - xl, n2, op)

            for h in range(2):
                hops = y if h == 0 else (4 - y) % 4
                e = t - 2 * hops - 2
                c = e % 16
                first = c < 8
                k = jnp.where(first, xh, 1 - xh)
                s, r = (c % 8) // 4, c % 4

                @pl.when(both(both(e >= 0, e < 16), (y != 0) | (k != xh)))
                def _():
                    i = (k * 2 + s) * 4 + r
                    if op:
                        arrived(cpiece(k, h, s, r), c_rec.at[h, i])
                    c_next(k, h, s, r, cpiece(k, h, s, r), op)
                    c_sib(k, h, s, r, op)

        loop(16 + 14 + 2, step)

    source_copies(True)

    def f_all(f):
        def rows(b):
            lax.fori_loop(b, NB, lambda c, s: (f(b, c), s)[1], 0)

        loop(NB, rows)

    @pl.when(is_root)
    def _():
        d_loc.start()
        d_loc.wait()
        lanes = lax.broadcasted_iota(jnp.int32, (8, B), 1)
        subs = lax.broadcasted_iota(jnp.int32, (8, B), 0)

        def factor(b):
            for v in range(NB):

                @pl.when(b == v)
                def _():
                    if v == 4:
                        arrived(dbuf.at[pl.ds(T, T), pl.ds(T, T)], d_rec.at[4])
                    s = dbuf[v * B : (v + 1) * B, v * B : (v + 1) * B]
                    if v:
                        u = fbuf[: v * B, v * B : (v + 1) * B]
                        s = s - mm(u, u, ((0,), (0,)), HI)
                    sbuf[:, :B] = s

            a = [sbuf[8 * h : 8 * h + 8, 0:B] for h in range(16)]
            w = [jnp.where(lanes == subs + 8 * h, 1.0, 0.0) for h in range(16)]
            o = base(a, w)
            for v in range(NB):

                @pl.when(b == v)
                def _():
                    for h in range(16):
                        fbuf[v * B + 8 * h : v * B + 8 * h + 8, v * B : (v + 1) * B] = o[h]
                    if v < 4:
                        arrived(dbuf.at[pl.ds(v * B, B), pl.ds(T, T)], d_rec.at[v])
                    if v < NB - 1:
                        s = dbuf[v * B : (v + 1) * B, (v + 1) * B :]
                        if v:
                            s = s - mm(
                                fbuf[: v * B, v * B : (v + 1) * B], fbuf[: v * B, (v + 1) * B :], ((0,), (0,)), HI
                            )
                        wv = fbuf[v * B : (v + 1) * B, v * B : (v + 1) * B]
                        fbuf[v * B : (v + 1) * B, (v + 1) * B :] = mm(wv, s, precision=HI)

            lax.fori_loop(b, NB, lambda c, s: (f_send(b, c, True), s)[1], 0)

        loop(NB, factor)

    @pl.when(both(d == 1, jnp.logical_not(is_root)))
    def _():
        def pass_on(b, c):
            arrived(fpiece(b, c), f_rec.at[b * NB + c])
            f_send(b, c, True)

        f_all(pass_on)

    @pl.when(d == 0)
    def _():
        forward(True)
        f_all(lambda b, c: arrived(fpiece(b, c), f_rec.at[b * NB + c]))

    @pl.when(d == 1)
    def _():
        def one(n):
            @pl.when(z != 0)
            def _():
                arrived(rpiece(xl, n), r_rec.at[xl, n])

            arrived(rpiece(1 - xl, n), r_rec.at[1 - xl, n])

        loop(RN, one)

        def two(i):
            k, s, r = i // 8, (i % 8) // 4, i % 4

            @pl.when((y != 0) | (k != xh))
            def _():
                arrived(cpiece(k, 1, s, r), c_rec.at[1, i])

        loop(16, two)

    @pl.when(src_r)
    def _():
        r_loc.wait()

    @pl.when(src_c)
    def _():
        for c in c_loc:
            c.wait()

    G = 256
    crow = pl.ds(pl.multiple_of(d * T, 8), T)
    for g in range(2 * T // G):
        at = g * G
        w1 = fbuf[at : at + B, at : at + B]
        w2 = fbuf[at + B : at + G, at + B : at + G]
        u12 = fbuf[at : at + B, at + B : at + G]
        w21 = -mm(w2, mm(u12, w1, ((0,), (0,)), HI), precision=HI)
        wbuf[:B, :B] = w1
        wbuf[:B, B:] = jnp.zeros((B, B), F32)
        wbuf[B:, :B] = w21
        wbuf[B:, B:] = w2
        w = split(wbuf[...])
        wt = split(wbuf[...].T)
        if g:
            uf = fbuf[:at, at : at + G]
            u = split(uf)
            ut = split(uf.T)
        acc = cbuf[crow, at : at + G]
        if g:
            acc = acc - mm3((lh[:, :at], ll[:, :at]), u)
        a, b = split(mm3(split(acc), wt))
        lh[:, at : at + G] = a
        ll[:, at : at + G] = b

        def columns(n):
            cols = pl.ds(pl.multiple_of(n * T, B), T)
            acc = rbuf[at : at + G, cols]
            if g:
                acc = acc - mm3(ut, (vh[:at, cols], vl[:at, cols]))
            a, b = split(mm3(w, split(acc)))
            vh[at : at + G, cols] = a
            vl[at : at + G, cols] = b

        loop(4, columns)

    for c in own:
        c.wait()

    def store(n):
        return pltpu.make_async_copy(
            abuf.at[:, pl.ds(pl.multiple_of(n * T, B), T)],
            out.at[:, pl.ds(pl.multiple_of(n * T, B), T)],
            loc.at[6 + n],
        )

    def update(n):
        cols = pl.ds(pl.multiple_of(n * T, B), T)
        for s in range(2):
            rows = slice(s * 256, s * 256 + 256)
            res = abuf[rows, cols] - mm3((lh[rows, :], ll[rows, :]), (vh[:, cols], vl[:, cols]))
            if s == 0:
                res = jnp.where(p < 2, 0.0, res)
            abuf[rows, cols] = res

        @pl.when(both(n == 0, q < 2))
        def _():
            pick = pl.ds(pl.multiple_of(q * T, B), T)
            for s in range(2):
                rows = slice(s * 256, s * 256 + 256)
                res = lh[rows, pick].astype(F32) + ll[rows, pick].astype(F32)
                if s == 0:
                    i = lax.broadcasted_iota(jnp.int32, (256, T), 0) + d * 256
                    j = lax.broadcasted_iota(jnp.int32, (256, T), 1)
                    res = jnp.where((p > q) | ((p == q) & (i >= j)), res, 0.0)
                abuf[rows, 0:T] = res

        store(n).start()

    loop(4, update)
    loop(4, lambda n: store(n).wait())

    d_copies(False)
    source_copies(False)

    @pl.when(d == 0)
    def _():
        forward(False)

    @pl.when(d == 1)
    def _():
        f_all(lambda b, c: f_send(b, c, False))


def call(x):
    dma = pltpu.SemaphoreType.DMA
    return pl.pallas_call(
        kernel,
        out_shape=jax.ShapeDtypeStruct((T, 4 * T), F32),
        in_specs=[pl.BlockSpec(memory_space=pl.ANY)],
        out_specs=pl.BlockSpec(memory_space=pl.ANY),
        scratch_shapes=[
            pltpu.VMEM((2 * T, 4 * T), F32),
            pltpu.VMEM((2 * T, 2 * T), F32),
            pltpu.VMEM((2 * T, 2 * T), F32),
            pltpu.VMEM((2 * T, 2 * T), F32),
            pltpu.VMEM((T, 4 * T), F32),
            pltpu.VMEM((2 * T, 4 * T), BF16),
            pltpu.VMEM((2 * T, 4 * T), BF16),
            pltpu.VMEM((T, 2 * T), BF16),
            pltpu.VMEM((T, 2 * T), BF16),
            pltpu.VMEM((256, 256), F32),
            pltpu.VMEM((B, B), F32),
            dma((2, RN)),
            dma((2, 16)),
            dma((NB * NB,)),
            dma((5,)),
            dma((RN,)),
            dma((RN,)),
            dma((2, RN)),
            dma((2, 16)),
            dma((2, 16)),
            dma((16,)),
            dma((7, NB * NB)),
            dma((5,)),
            dma((10,)),
        ],
        compiler_params=pltpu.CompilerParams(has_side_effects=True, vmem_limit_bytes=56 * 1024 * 1024),
        name="panels",
    )(x)


def body(matrix):
    return call(matrix.reshape(2 * T, 4 * T)).reshape(2, 1, T // 2, 4, 1, T)


def solution(mesh):
    return jax.shard_map(
        body,
        mesh=mesh,
        in_specs=(P(None, "row", None, None, "col", None),),
        out_specs=P(None, "row", "depth", None, "col", None),
        check_vma=False,
    )
```

time: 1230 us -> 204 us (0.17)
  the two profiles are of different devices: /device:TPU:38 before, /device:TPU:12 now
where the time goes in v1:
time: 204 us
  Pallas kernels  159 us (78%)
  other arithmetic  26.5 us (13%)
  local copies, waits for them, and re-layouts  18.4 us (9%)
    pallas_call x1, Pallas kernels, call(): pl.pallas_call(kernel, out_shape=jax.ShapeDtypeStruct((T, 4 * T), F32), i...  159 us
    unnamed x1, other arithmetic  26.5 us
    unnamed x1, local copies, waits for them, and re-layouts  10.7 us
    reshape x1, local copies, waits for them, and re-layouts, body(): return call(matrix.reshape(2 * T, 4 * T)).reshape(2, 1, T // 2, 4, 1, T)  7.64 us

profile of v1, /device:TPU:12, one launch (start us, length us, event | category | flops | bytes accessed | tf_op | source)
XLA Modules:
  0.0 203.7 jit_solution(16705680293264666607)
XLA Ops:
  0.0 26.5 %reduce = f32[2,512,4,512]{3,2,1,0:T(4,128)} reduce(f32[2,1,512,4,1,512]{5,4,3,2,1,0:T(1,128)} %param.1, f32[]{:T(128)} %constant.1), dimensions={1,4}, to_apply=%param.1.reduce_sub_computation | reduce | bytes 16777220 | tf_op args[0]
  26.5 10.7 %copy.3 = f32[128,8,4,512]{3,1,2,0:T(8,128)} copy(f32[128,8,4,512]{3,2,1,0:T(4,128)} %bitcast.3) | data formatting | bytes 16777216
  37.2 158.8 %panels.1 = f32[512,2048]{1,0:T(8,128)} custom-call(f32[1024,2048]{1,0:T(8,128)} %bitcast.4), custom_call_target="tpu_custom_call" | custom-call | tf_op jit(solution)/shard_map/panels/pallas_call | solution.py:457
  196.1 7.6 %reshape.8 = f32[2,1,256,4,1,512]{5,4,3,2,1,0:T(1,128)} reshape(f32[512,2048]{1,0:T(8,128)} %panels.1) | data formatting | bytes 8388608 | tf_op jit(solution)/shard_map/reshape | solution.py:494

commit v2 on v1

v2 whole, which is shorter than its diff:
```python
import functools

import jax
import jax.numpy as jnp
from jax import lax
from jax.experimental import pallas as pl
from jax.experimental.pallas import tpu as pltpu
from jax.sharding import PartitionSpec as P

T = 512
B = 128
NB = 2 * T // B
RN = 32
RR = T // RN
CR = 64
L16 = 4 * T // B
SCHED = (8, 8, 8, 8)
HI = lax.Precision.HIGHEST
MESH = pl.DeviceIdType.MESH
F32 = jnp.float32
BF16 = jnp.bfloat16


def mm(a, b, dims=((1,), (0,)), precision=None):
    return lax.dot_general(a, b, (dims, ((), ())), precision=precision, preferred_element_type=F32)


def split(x):
    h = x.astype(BF16)
    return h, (x - h.astype(F32)).astype(BF16)


def mm3(a, b, dims=((1,), (0,))):
    return mm(a[0], b[0], dims) + (mm(a[0], b[1], dims) + mm(a[1], b[0], dims))


def base(a, w):
    out = []
    sub = lax.broadcasted_iota(jnp.int32, (8, B), 0)
    lane = lambda x, k: jnp.broadcast_to(x[:, k : k + 1], (8, B))
    row = lambda x, m: jnp.broadcast_to(x[m : m + 1, :], (8, B))
    for g in range(16):
        cg = [lane(a[g], 8 * g + n) for n in range(8)]
        e = [[row(cg[n], m) if n >= m else None for n in range(8)] for m in range(8)]
        ar = [row(a[g], m) for m in range(8)]
        wr = [row(w[g], m) for m in range(8)]
        rs = [None] * 8
        u = [[None] * 8 for _ in range(8)]
        for m in range(8):
            rs[m] = lax.rsqrt(e[m][m])
            for n in range(m + 1, 8):
                u[m][n] = e[m][n] * rs[m]
            ar[m] = ar[m] * rs[m]
            wr[m] = wr[m] * rs[m]
            for m2 in range(m + 1, 8):
                for n in range(m2, 8):
                    e[m2][n] = e[m2][n] - u[m][m2] * u[m][n]
                ar[m2] = ar[m2] - u[m][m2] * ar[m]
                wr[m2] = wr[m2] - u[m][m2] * wr[m]
        o = wr[0]
        for m in range(1, 8):
            o = jnp.where(sub == m, wr[m], o)
        out.append(o)
        for h in range(g + 1, 16):
            c = [lane(a[h], 8 * g + n) for n in range(8)]
            for m in range(8):
                f = c[m] * rs[m]
                for n in range(m + 1, 8):
                    c[n] = c[n] - f * u[m][n]
                a[h] = a[h] - f * ar[m]
                w[h] = w[h] - f * wr[m]
    return out


def kernel(
    x, xq, abuf, rbuf, cbuf, fbuf, dbuf, vh, vl, lh, ll, wbuf, sbuf, part,
    r_rec, c_rec, f_rec, d_rec, rz_s, rx_s, rs_s, cy_s, cx_s, cs_s, f_s, d_s, loc,
):
    p, q, d = lax.axis_index("row"), lax.axis_index("col"), lax.axis_index("depth")
    z, xl = p // 2, p % 2
    y, xh = q // 2, q % 2
    xx = xh * 2 + xl
    dev = lambda zz, xli, yy, xhi, dd: (zz * 2 + xli, yy * 2 + xhi, dd)
    sib = dev(z, xl, y, xh, 1 - d)
    both = jnp.logical_and

    def remote(src, dst, ssem, rsem, to):
        return pltpu.make_async_remote_copy(
            src_ref=src, dst_ref=dst, send_sem=ssem, recv_sem=rsem, device_id=to, device_id_type=MESH
        )

    def arrived(dst, rsem):
        pltpu.make_async_copy(dst, dst, rsem).wait()

    def when_start(cond, copy, op):
        @pl.when(cond)
        def _():
            c = copy()
            c.start() if op else c.wait_send()

    is_root = both(both(p == 0, q == 0), d == 1)
    src_r = z == 0
    src_c = y == 0

    own = [
        pltpu.make_async_copy(
            x.at[pl.ds(pl.multiple_of((s * T + d * 256) * L16, 8), 256 * L16), :],
            abuf.at[pl.ds(s * 256 * L16, 256 * L16), :],
            loc.at[s],
        )
        for s in range(2)
    ]
    for c in own:
        c.start()
    r_loc = pltpu.make_async_copy(
        x.at[pl.ds(0, T * L16), :], rbuf.at[pl.ds(pl.multiple_of(xl * T * L16, 8), T * L16), :], loc.at[2]
    )
    c_loc = [
        pltpu.make_async_copy(
            xq.at[pl.ds(s * T + d * 256, 256), 0], cbuf.at[xh, pl.ds(d * T + s * 256, 256)], loc.at[3 + s]
        )
        for s in range(2)
    ]
    d_loc = pltpu.make_async_copy(xq.at[pl.ds(0, T), 0], dbuf.at[0, pl.ds(0, T)], loc.at[5])

    @pl.when(src_r)
    def _():
        r_loc.start()

    @pl.when(src_c)
    def _():
        for c in c_loc:
            c.start()

    @pl.when(is_root)
    def _():
        d_loc.start()

    near = [
        sib,
        dev((z + 1) % 8, xl, y, xh, d), dev((z + 7) % 8, xl, y, xh, d),
        dev(z, xl, (y + 1) % 4, xh, d), dev(z, xl, (y + 3) % 4, xh, d),
        dev(z, 1 - xl, y, xh, d), dev(z, xl, y, 1 - xh, d), dev(z, 1 - xl, y, 1 - xh, d),
    ]
    barrier = pltpu.get_barrier_semaphore()
    for to in near:
        pl.semaphore_signal(barrier, inc=1, device_id=to, device_id_type=MESH)
    pl.semaphore_wait(barrier, len(near))

    rpiece = lambda k, n: rbuf.at[pl.ds(pl.multiple_of((k * T + n * RR) * L16, 8), RR * L16), :]
    xr = lambda n: x.at[pl.ds(pl.multiple_of(n * RR * L16, 8), RR * L16), :]

    def cpiece(k, h, s, r):
        return cbuf.at[k, pl.ds(h * T + s * 256 + r * CR, CR)]

    xc = lambda h, s, r: xq.at[pl.ds(s * T + h * 256 + r * CR, CR), 0]
    fpiece = lambda b, c: fbuf.at[pl.ds(pl.multiple_of(b * B, B), B), pl.ds(pl.multiple_of(c * B, B), B)]

    def r_own(n, src, op):
        up = n % 2 == 0
        nxt = jnp.where(up, (z + 1) % 8, (z + 7) % 8)
        more = jnp.where(up, z != 7, z != 1)
        when_start(
            more, lambda: remote(src, rpiece(xl, n), rz_s.at[n], r_rec.at[xl, n], dev(nxt, xl, y, xh, 0)), op
        )
        when_start(
            z >= 0, lambda: remote(src, rpiece(xl, n), rx_s.at[n], r_rec.at[xl, n], dev(z, 1 - xl, y, xh, 0)), op
        )

    def r_sib(k, n, op):
        when_start(
            z >= 0, lambda: remote(rpiece(k, n), rpiece(k, n), rs_s.at[k, n], r_rec.at[k, n], sib), op
        )

    def c_next(k, h, s, r, src, more, op):
        i = (k * 2 + s) * 4 + r
        nxt = jnp.where(h == 0, (y + 1) % 4, (y + 3) % 4)
        when_start(
            more, lambda: remote(src, cpiece(k, h, s, r), cy_s.at[h, i], c_rec.at[h, i], dev(z, xl, nxt, xh, 0)), op
        )

    def c_cross(k, h, s, r, src, op):
        i = (k * 2 + s) * 4 + r
        when_start(
            y == (r + 2 * h) % 4,
            lambda: remote(src, cpiece(k, h, s, r), cx_s.at[h, i], c_rec.at[h, i], dev(z, xl, y, 1 - xh, 0)), op,
        )

    def c_sib(k, h, s, r, op):
        i = (k * 2 + s) * 4 + r
        when_start(
            h == 1,
            lambda: remote(cpiece(k, h, s, r), cpiece(k, h, s, r), cs_s.at[i], c_rec.at[h, i], sib), op,
        )

    def f_send(b, c, op):
        v = fpiece(b, c)
        i = b * NB + c
        go = lambda cond, slot, to: when_start(
            cond, lambda: remote(v, v, f_s.at[slot, i], f_rec.at[i], to), op
        )
        root_line = both(z == 0, y == 0)
        go(both(root_line, xx == 0), 0, dev(z, 1, y, 0, 1))
        go(both(root_line, xx == 0), 1, dev(z, 1, y, 1, 1))
        go(both(root_line, xx == 1), 1, dev(z, 0, y, 1, 1))
        plane = y == 0
        go(both(plane, z <= 3), 2, dev((z + 1) % 8, xl, y, xh, 1))
        go(both(plane, (z == 0) | (z >= 6)), 3, dev((z + 7) % 8, xl, y, xh, 1))
        go((y == 0) | (y == 1), 4, dev(z, xl, (y + 1) % 4, xh, 1))
        go(y == 0, 5, dev(z, xl, (y + 3) % 4, xh, 1))
        go(z >= 0, 6, sib)

    def loop(n, f):
        lax.fori_loop(0, n, lambda i, s: (f(i), s)[1], 0)

    def d_copies(op):
        for i in range(4):
            when_start(
                both(both(p == 0, q == 1), d == 1),
                lambda: remote(
                    xq.at[pl.ds(i * B, B), 0], dbuf.at[1, pl.ds(i * B, B)], d_s.at[i], d_rec.at[i], (0, 0, 1)
                ),
                op,
            )
        when_start(
            both(both(p == 1, q == 1), d == 1),
            lambda: remote(
                xq.at[pl.ds(0, T), 0], dbuf.at[1, pl.ds(T, T)], d_s.at[4], d_rec.at[4], (0, 0, 1)
            ),
            op,
        )

    d_copies(True)

    def source_copies(op):
        @pl.when(both(src_c, d == 0))
        def _():
            def one(i):
                s, r = i // 4, i % 4
                for h in range(2):
                    c_next(xh, h, s, r, xc(h, s, r), z >= 0, op)
                    c_cross(xh, h, s, r, xc(h, s, r), op)

            loop(8, one)

        @pl.when(both(src_r, d == 0))
        def _():
            loop(RN, lambda n: r_own(n, xr(n), op))

    def forward(op):
        def own_line(t):
            for up in range(2):
                hops = z if up == 0 else 8 - z
                e = t - 3 * hops
                n = 2 * e + up

                @pl.when(both(both(e >= 0, e < RN // 2), z != 0))
                def _():
                    if op:
                        arrived(rpiece(xl, n), r_rec.at[xl, n])
                    r_own(n, rpiece(xl, n), op)
                    r_sib(xl, n, op)

            for h in range(2):
                hops = y if h == 0 else (4 - y) % 4
                e = t - 3 * hops
                on = z >= 0

                @pl.when(both(both(e >= 0, e < 8), both(y != 0, on)))
                def _():
                    s, r = e // 4, e % 4
                    if op:
                        arrived(cpiece(xh, h, s, r), c_rec.at[h, (xh * 2 + s) * 4 + r])
                    c_next(xh, h, s, r, cpiece(xh, h, s, r), hops != 3, op)
                    c_cross(xh, h, s, r, cpiece(xh, h, s, r), op)
                    c_sib(xh, h, s, r, op)

        loop(max(RN // 2 + 7 * 3, 8 * 1 + 3 * 3), own_line)

        def other_line(j):
            for h in range(2):
                r = (y + j + 2 * h) % 4 if h else (y - j + 4) % 4
                for s in range(2):
                    k = 1 - xh
                    if op:
                        arrived(cpiece(k, h, s, r), c_rec.at[h, (k * 2 + s) * 4 + r])
                    c_next(k, h, s, r, cpiece(k, h, s, r), j != 3, op)
                    c_sib(k, h, s, r, op)

        loop(4, other_line)

        def across(t):
            for up in range(2):
                hops = z if up == 0 else 8 - z
                e = t - 3 * jnp.where(z == 0, 0, hops)
                n = 2 * e + up

                @pl.when(both(e >= 0, e < RN // 2))
                def _():
                    if op:
                        arrived(rpiece(1 - xl, n), r_rec.at[1 - xl, n])
                    r_sib(1 - xl, n, op)

        loop(RN // 2 + 7 * 3, across)

    source_copies(True)

    @pl.when(is_root)
    def _():
        d_loc.wait()
        lanes = lax.broadcasted_iota(jnp.int32, (8, B), 1)
        subs = lax.broadcasted_iota(jnp.int32, (8, B), 0)

        def dblock(v, c):
            return dbuf[c // 4, v * B : (v + 1) * B, c % 4, :]

        def factor(b):
            for v in range(NB):

                @pl.when(b == v)
                def _():
                    if v == 4:
                        arrived(dbuf.at[1, pl.ds(T, T)], d_rec.at[4])
                    s = dblock(v, v)
                    if v:
                        u = fbuf[: v * B, v * B : (v + 1) * B]
                        s = s - mm(u, u, ((0,), (0,)), HI)
                    sbuf[:, :B] = s

            a = [sbuf[8 * h : 8 * h + 8, 0:B] for h in range(16)]
            w = [jnp.where(lanes == subs + 8 * h, 1.0, 0.0) for h in range(16)]
            o = base(a, w)
            for v in range(NB):

                @pl.when(b == v)
                def _():
                    for h in range(16):
                        fbuf[v * B + 8 * h : v * B + 8 * h + 8, v * B : (v + 1) * B] = o[h]
                    if v < 4:
                        arrived(dbuf.at[1, pl.ds(v * B, B)], d_rec.at[v])
                    if v < NB - 1:
                        s = jnp.concatenate([dblock(v, c) for c in range(v + 1, NB)], axis=1)
                        if v:
                            s = s - mm(
                                fbuf[: v * B, v * B : (v + 1) * B], fbuf[: v * B, (v + 1) * B :], ((0,), (0,)), HI
                            )
                        wv = fbuf[v * B : (v + 1) * B, v * B : (v + 1) * B]
                        fbuf[v * B : (v + 1) * B, (v + 1) * B :] = mm(wv, s, precision=HI)

            lax.fori_loop(b, NB, lambda c, s: (f_send(b, c, True), s)[1], 0)

        loop(NB, factor)

    @pl.when(d == 0)
    def _():
        forward(True)

    passes = both(d == 1, jnp.logical_not(is_root))

    def pass_on(b, c):
        arrived(fpiece(b, c), f_rec.at[b * NB + c])
        f_send(b, c, True)

    def take(b, c):
        arrived(fpiece(b, c), f_rec.at[b * NB + c])

    def f_rows(first, last, f):
        def rows(b, _):
            lax.fori_loop(b, NB, lambda c, s: (f(b, c), s)[1], 0)
            return 0

        lax.fori_loop(first, last, rows, 0)

    def panels_here(k, half):
        @pl.when(d == 1)
        def _():
            def one(i):
                n = half * (RN // 2) + i

                @pl.when((z != 0) | (k != xl))
                def _():
                    arrived(rpiece(k, n), r_rec.at[k, n])

            loop(RN // 2, one)

            def two(i):
                @pl.when((y != 0) | (k != xh))
                def _():
                    arrived(cpiece(k, 1, i // 4, i % 4), c_rec.at[1, k * 8 + i])

            if half == 0:
                loop(8, two)

        if half == 0:

            @pl.when(both(src_r, k == xl))
            def _():
                r_loc.wait()

            @pl.when(both(src_c, k == xh))
            def _():
                for c in c_loc:
                    c.wait()

    G = 256
    crow = pl.ds(d * T, T)

    def rload(at, n):
        return jnp.concatenate([rbuf[pl.ds(at * L16 + n * 4 + c, G, stride=L16), :] for c in range(4)], axis=1)

    def aload(s, n):
        return jnp.concatenate(
            [abuf[pl.ds(s * 256 * L16 + n * 4 + c, 256, stride=L16), :] for c in range(4)], axis=1
        )

    def astore(s, n, val):
        for c in range(4):
            abuf[pl.ds(s * 256 * L16 + n * 4 + c, 256, stride=L16), :] = val[:, c * B : (c + 1) * B]

    for g in range(2 * T // G):
        at = g * G
        if SCHED[g] > (SCHED[g - 1] if g else 0):

            @pl.when(passes)
            def _():
                f_rows(SCHED[g - 1] if g else 0, SCHED[g], pass_on)

        panels_here(g // 2, g % 2)
        if g == 0:
            for c in own:
                c.wait()
        c4 = (at % T) // B
        acc = jnp.concatenate([cbuf[g // 2, crow, c4 + c, :] for c in range(2)], axis=1)
        if g:
            uf = fbuf[:at, at : at + G]
            u = split(uf)
            ut = split(uf.T)
            acc = acc - mm3((lh[:, :at], ll[:, :at]), u)

            def before(n):
                cols = pl.ds(pl.multiple_of(n * T, B), T)
                part[:, cols] = rload(at, n) - mm3(ut, (vh[:at, cols], vl[:at, cols]))

            loop(4, before)
        wbuf[:, :G] = acc

        @pl.when(d == 0)
        def _():
            f_rows(2 * g, 2 * g + 2, take)

        w1 = fbuf[at : at + B, at : at + B]
        w2 = fbuf[at + B : at + G, at + B : at + G]
        u12 = fbuf[at : at + B, at + B : at + G]
        w21 = -mm(w2, mm(u12, w1, ((0,), (0,)), HI), precision=HI)
        w = jnp.concatenate(
            [jnp.concatenate([w1, jnp.zeros((B, B), F32)], axis=1), jnp.concatenate([w21, w2], axis=1)], axis=0
        )
        wt = split(w.T)
        w = split(w)
        a, b = split(mm3(split(wbuf[...]), wt))
        lh[:, at : at + G] = a
        ll[:, at : at + G] = b

        def columns(n):
            cols = pl.ds(pl.multiple_of(n * T, B), T)
            a, b = split(mm3(w, split(part[:, cols] if g else rload(at, n))))
            vh[at : at + G, cols] = a
            vl[at : at + G, cols] = b
            for s in range(2):
                rows = slice(s * 256, s * 256 + 256)
                res = aload(s, n) - mm3((lh[rows, at : at + G], ll[rows, at : at + G]), (a, b))
                if s == 0 and g == 3:
                    res = jnp.where(p < 2, 0.0, res)
                astore(s, n, res)

        loop(4, columns)

    @pl.when(q < 2)
    def _():
        pick = pl.ds(pl.multiple_of(q * T, B), T)
        for s in range(2):
            rows = slice(s * 256, s * 256 + 256)
            res = lh[rows, pick].astype(F32) + ll[rows, pick].astype(F32)
            if s == 0:
                i = lax.broadcasted_iota(jnp.int32, (256, T), 0) + d * 256
                j = lax.broadcasted_iota(jnp.int32, (256, T), 1)
                res = jnp.where((p > q) | ((p == q) & (i >= j)), res, 0.0)
            astore(s, 0, res)

    d_copies(False)
    source_copies(False)

    @pl.when(d == 0)
    def _():
        forward(False)

    @pl.when(d == 1)
    def _():
        f_rows(0, NB, lambda b, c: f_send(b, c, False))


def call(x, xq):
    dma = pltpu.SemaphoreType.DMA
    return pl.pallas_call(
        kernel,
        out_shape=pltpu.VMEM((T * L16, B), F32),
        in_specs=[pl.BlockSpec(memory_space=pltpu.HBM)] * 2,
        out_specs=pl.BlockSpec(memory_space=pltpu.VMEM),
        scratch_shapes=[
            pltpu.VMEM((2 * T * L16, B), F32),
            pltpu.VMEM((2, 2 * T, 4, B), F32),
            pltpu.VMEM((2 * T, 2 * T), F32),
            pltpu.VMEM((2, 2 * T, 4, B), F32),
            pltpu.VMEM((2 * T, 4 * T), BF16),
            pltpu.VMEM((2 * T, 4 * T), BF16),
            pltpu.VMEM((T, 2 * T), BF16),
            pltpu.VMEM((T, 2 * T), BF16),
            pltpu.VMEM((T, 256), F32),
            pltpu.VMEM((B, B), F32),
            pltpu.VMEM((256, 4 * T), F32),
            dma((2, RN)),
            dma((2, 16)),
            dma((NB * NB,)),
            dma((5,)),
            dma((RN,)),
            dma((RN,)),
            dma((2, RN)),
            dma((2, 16)),
            dma((2, 16)),
            dma((16,)),
            dma((7, NB * NB)),
            dma((5,)),
            dma((7,)),
        ],
        compiler_params=pltpu.CompilerParams(collective_id=0, has_side_effects=True, vmem_limit_bytes=56 * 1024 * 1024),
        name="panels",
    )(x, xq)


def body(matrix):
    out = call(matrix.reshape(2 * T * L16, B), matrix.reshape(2 * T, 4, 4, B))
    return out.reshape(2, 1, T // 2, 4, 1, T)


def solution(mesh):
    return jax.shard_map(
        body,
        mesh=mesh,
        in_specs=(P(None, "row", None, None, "col", None),),
        out_specs=P(None, "row", "depth", None, "col", None),
        check_vma=False,
    )
```

time: 204 us -> 140 us (0.69)
  the two profiles are of different devices: /device:TPU:12 before, /device:TPU:38 now
where the time goes in v2:
time: 140 us; the launch traced here: 138 us
  Pallas kernels  136 us (97%)
  local copies, waits for them, and re-layouts  2.02 us (1%)
    pallas_call x1, Pallas kernels, call(): pl.pallas_call(kernel, out_shape=pltpu.VMEM((T * L16, B), F32), in_specs=...  136 us

profile of v2, /device:TPU:38, one launch (start us, length us, event | category | flops | bytes accessed | tf_op | source)
XLA Modules:
  0.0 137.6 jit_solution(6609477327626992927)
XLA Ops:
  0.0 135.6 %panels.1 = f32[8192,128]{1,0:T(8,128)S(1)} custom-call(f32[16384,128]{1,0:T(8,128)} %bitcast.4, f32[1024,4,4,128]{3,2,1,0:T(4,128)} %bitcast.5), custom_call_target="tpu_custom_call" | custom-call | tf_op jit(solution)/shard_map/panels/pallas_call | solution.py:504
  135.6 2.0 %copy.4 = f32[2,1,256,4,1,512]{5,4,3,2,1,0:T(1,128)} copy(f32[2,1,256,4,1,512]{5,4,3,2,1,0:T(1,128)S(1)} %bitcast.3) | data formatting | bytes 8388608

commit v3 on v2

--- a/solution.py
+++ b/solution.py
@@ -73,7 +73,7 @@
 
 
 def kernel(
-    x, xq, abuf, rbuf, cbuf, fbuf, dbuf, vh, vl, lh, ll, wbuf, sbuf, part,
+    x, xq, abuf, rbuf, cbuf, fbuf, dbuf, vh, vl, lh, ll, wbuf, sbuf, part, vx, v_s, v_rec,
     r_rec, c_rec, f_rec, d_rec, rz_s, rx_s, rs_s, cy_s, cx_s, cs_s, f_s, d_s, loc,
 ):
     p, q, d = lax.axis_index("row"), lax.axis_index("col"), lax.axis_index("depth")
@@ -156,16 +156,12 @@
     xc = lambda h, s, r: xq.at[pl.ds(s * T + h * 256 + r * CR, CR), 0]
     fpiece = lambda b, c: fbuf.at[pl.ds(pl.multiple_of(b * B, B), B), pl.ds(pl.multiple_of(c * B, B), B)]
 
-    def r_own(n, src, op):
-        up = n % 2 == 0
-        nxt = jnp.where(up, (z + 1) % 8, (z + 7) % 8)
-        more = jnp.where(up, z != 7, z != 1)
-        when_start(
-            more, lambda: remote(src, rpiece(xl, n), rz_s.at[n], r_rec.at[xl, n], dev(nxt, xl, y, xh, 0)), op
-        )
-        when_start(
-            z >= 0, lambda: remote(src, rpiece(xl, n), rx_s.at[n], r_rec.at[xl, n], dev(z, 1 - xl, y, xh, 0)), op
-        )
+    def r_ring(n, src):
+        nxt = jnp.where(n % 2 == 0, (z + 1) % 8, (z + 7) % 8)
+        return remote(src, rpiece(xl, n), rz_s.at[n], r_rec.at[xl, n], dev(nxt, xl, y, xh, 0))
+
+    def r_cross(n, src):
+        return remote(src, rpiece(xl, n), rx_s.at[n], r_rec.at[xl, n], dev(z, 1 - xl, y, xh, 0))
 
     def r_sib(k, n, op):
         when_start(
@@ -243,22 +239,44 @@
 
             loop(8, one)
 
-        @pl.when(both(src_r, d == 0))
-        def _():
-            loop(RN, lambda n: r_own(n, xr(n), op))
-
     def forward(op):
         def own_line(t):
+            if op:
+                @pl.when(z == 0)
+                def _():
+                    @pl.when(t < RN // 2)
+                    def _():
+                        for up in range(2):
+                            r_ring(2 * t + up, xr(2 * t + up)).start()
+
+                    @pl.when(t < RN)
+                    def _():
+                        r_cross(t, xr(t)).start()
+
+                    o = t - 3
+
+                    @pl.when(both(o >= 0, o < RN // 2))
+                    def _():
+                        for up in range(2):
+                            r_ring(2 * o + up, xr(2 * o + up)).wait_send()
+
+                    @pl.when(both(o >= 0, o < RN))
+                    def _():
+                        r_cross(o, xr(o)).wait_send()
+
             for up in range(2):
                 hops = z if up == 0 else 8 - z
-                e = t - 3 * hops
+                last = (z == 7) if up == 0 else (z == 1)
+                first = 3 * hops
+                e = t - first
                 n = 2 * e + up
 
                 @pl.when(both(both(e >= 0, e < RN // 2), z != 0))
                 def _():
                     if op:
                         arrived(rpiece(xl, n), r_rec.at[xl, n])
-                    r_own(n, rpiece(xl, n), op)
+                    when_start(jnp.logical_not(last), lambda: r_ring(n, rpiece(xl, n)), op)
+                    when_start(z >= 0, lambda: r_cross(n, rpiece(xl, n)), op)
                     r_sib(xl, n, op)
 
             for h in range(2):
@@ -274,8 +292,6 @@
                     c_next(xh, h, s, r, cpiece(xh, h, s, r), hops != 3, op)
                     c_cross(xh, h, s, r, cpiece(xh, h, s, r), op)
                     c_sib(xh, h, s, r, op)
-
-        loop(max(RN // 2 + 7 * 3, 8 * 1 + 3 * 3), own_line)
 
         def other_line(j):
             for h in range(2):
@@ -287,21 +303,24 @@
                     c_next(k, h, s, r, cpiece(k, h, s, r), j != 3, op)
                     c_sib(k, h, s, r, op)
 
-        loop(4, other_line)
-
-        def across(t):
-            for up in range(2):
-                hops = z if up == 0 else 8 - z
-                e = t - 3 * jnp.where(z == 0, 0, hops)
-                n = 2 * e + up
-
-                @pl.when(both(e >= 0, e < RN // 2))
-                def _():
-                    if op:
-                        arrived(rpiece(1 - xl, n), r_rec.at[1 - xl, n])
-                    r_sib(1 - xl, n, op)
-
-        loop(RN // 2 + 7 * 3, across)
+        def step(t):
+            own_line(t)
+            for j in range(4):
+
+                @pl.when(t == 20 + 4 * j)
+                def _():
+                    other_line(j)
+
+        loop(5 + RN, step)
+
+    def across(half, op):
+        def one(i):
+            n = half * (RN // 2) + i
+            if op:
+                arrived(rpiece(1 - xl, n), r_rec.at[1 - xl, n])
+            r_sib(1 - xl, n, op)
+
+        loop(RN // 2, one)
 
     source_copies(True)
 
@@ -408,6 +427,11 @@
     def rload(at, n):
         return jnp.concatenate([rbuf[pl.ds(at * L16 + n * 4 + c, G, stride=L16), :] for c in range(4)], axis=1)
 
+    def v_copy(g, i):
+        n = 2 * d + i
+        v = vx.at[pl.ds(g * G, G), pl.ds(pl.multiple_of(n * T, B), T)]
+        return remote(v, v, v_s.at[g * 2 + i], v_rec.at[g * 4 + n], sib)
+
     def aload(s, n):
         return jnp.concatenate(
             [abuf[pl.ds(s * 256 * L16 + n * 4 + c, 256, stride=L16), :] for c in range(4)], axis=1
@@ -424,6 +448,12 @@
             @pl.when(passes)
             def _():
                 f_rows(SCHED[g - 1] if g else 0, SCHED[g], pass_on)
+
+        if g < 2:
+
+            @pl.when(d == 0)
+            def _():
+                across(g, True)
 
         panels_here(g // 2, g % 2)
         if g == 0:
@@ -437,11 +467,12 @@
             ut = split(uf.T)
             acc = acc - mm3((lh[:, :at], ll[:, :at]), u)
 
-            def before(n):
+            def before(i):
+                n = 2 * d + i
                 cols = pl.ds(pl.multiple_of(n * T, B), T)
                 part[:, cols] = rload(at, n) - mm3(ut, (vh[:at, cols], vl[:at, cols]))
 
-            loop(4, before)
+            loop(2, before)
         wbuf[:, :G] = acc
 
         @pl.when(d == 0)
@@ -457,23 +488,43 @@
         )
         wt = split(w.T)
         w = split(w)
-        a, b = split(mm3(split(wbuf[...]), wt))
-        lh[:, at : at + G] = a
-        ll[:, at : at + G] = b
-
-        def columns(n):
+
+        def solve(i):
+            n = 2 * d + i
             cols = pl.ds(pl.multiple_of(n * T, B), T)
-            a, b = split(mm3(w, split(part[:, cols] if g else rload(at, n))))
+            v = mm3(w, split(part[:, cols] if g else rload(at, n)))
+            vx[at : at + G, cols] = v
+            a, b = split(v)
             vh[at : at + G, cols] = a
             vl[at : at + G, cols] = b
-            for s in range(2):
-                rows = slice(s * 256, s * 256 + 256)
-                res = aload(s, n) - mm3((lh[rows, at : at + G], ll[rows, at : at + G]), (a, b))
-                if s == 0 and g == 3:
-                    res = jnp.where(p < 2, 0.0, res)
-                astore(s, n, res)
-
-        loop(4, columns)
+            v_copy(g, i).start()
+
+        loop(2, solve)
+        la, lb = split(mm3(split(wbuf[...]), wt))
+        lh[:, at : at + G] = la
+        ll[:, at : at + G] = lb
+
+    def there(i):
+        rows = pl.ds(pl.multiple_of((i // 2) * G, G), G)
+        n = 2 * (1 - d) + i % 2
+        cols = pl.ds(pl.multiple_of(n * T, B), T)
+        arrived(vx.at[rows, cols], v_rec.at[(i // 2) * 4 + n])
+        a, b = split(vx[rows, cols])
+        vh[rows, cols] = a
+        vl[rows, cols] = b
+
+    loop(8, there)
+
+    def update(n):
+        cols = pl.ds(pl.multiple_of(n * T, B), T)
+        for s in range(2):
+            rows = slice(s * 256, s * 256 + 256)
+            res = aload(s, n) - mm3((lh[rows, :], ll[rows, :]), (vh[:, cols], vl[:, cols]))
+            if s == 0:
+                res = jnp.where(p < 2, 0.0, res)
+            astore(s, n, res)
+
+    loop(4, update)
 
     @pl.when(q < 2)
     def _():
@@ -487,12 +538,16 @@
                 res = jnp.where((p > q) | ((p == q) & (i >= j)), res, 0.0)
             astore(s, 0, res)
 
+    for g in range(4):
+        loop(2, lambda i: v_copy(g, i).wait_send())
     d_copies(False)
     source_copies(False)
 
     @pl.when(d == 0)
     def _():
         forward(False)
+        across(0, False)
+        across(1, False)
 
     @pl.when(d == 1)
     def _():
@@ -518,6 +573,9 @@
             pltpu.VMEM((T, 256), F32),
             pltpu.VMEM((B, B), F32),
             pltpu.VMEM((256, 4 * T), F32),
+            pltpu.VMEM((2 * T, 4 * T), F32),
+            dma((8,)),
+            dma((16,)),
             dma((2, RN)),
             dma((2, 16)),
             dma((NB * NB,)),

time: 140 us -> 129 us (0.921); the launches traced: 138 us -> 129 us
  Pallas kernels: 136 us -> 127 us
    pallas_call x1, Pallas kernels: 136 us -> 127 us  [call(): pl.pallas_call(kernel, out_shape=pltpu.VMEM((T * L16, B), F32), in_specs=...]
where the time goes in v3:
time: 129 us
  Pallas kernels  127 us (98%)
  local copies, waits for them, and re-layouts  2.02 us (2%)
    pallas_call x1, Pallas kernels, call(): pl.pallas_call(kernel, out_shape=pltpu.VMEM((T * L16, B), F32), in_specs=...  127 us

profile of v3, /device:TPU:38, one launch (start us, length us, event | category | flops | bytes accessed | tf_op | source)
XLA Modules:
  0.0 129.1 jit_solution(3375942279134673638)
XLA Ops:
  0.0 127.0 %panels.1 = f32[8192,128]{1,0:T(8,128)S(1)} custom-call(f32[16384,128]{1,0:T(8,128)} %bitcast.4, f32[1024,4,4,128]{3,2,1,0:T(4,128)} %bitcast.5), custom_call_target="tpu_custom_call" | custom-call | tf_op jit(solution)/shard_map/panels/pallas_call | solution.py:559
  127.1 2.0 %copy.4 = f32[2,1,256,4,1,512]{5,4,3,2,1,0:T(1,128)} copy(f32[2,1,256,4,1,512]{5,4,3,2,1,0:T(1,128)S(1)} %bitcast.3) | data formatting | bytes 8388608

commit v4 on v3

--- a/solution.py
+++ b/solution.py
@@ -228,16 +228,13 @@
 
     d_copies(True)
 
-    def source_copies(op):
+    def c_source(i, op):
         @pl.when(both(src_c, d == 0))
         def _():
-            def one(i):
-                s, r = i // 4, i % 4
-                for h in range(2):
-                    c_next(xh, h, s, r, xc(h, s, r), z >= 0, op)
-                    c_cross(xh, h, s, r, xc(h, s, r), op)
-
-            loop(8, one)
+            s, r = i // 4, i % 4
+            for h in range(2):
+                c_next(xh, h, s, r, xc(h, s, r), z >= 0, op)
+                c_cross(xh, h, s, r, xc(h, s, r), op)
 
     def forward(op):
         def own_line(t):
@@ -253,16 +250,18 @@
                     def _():
                         r_cross(t, xr(t)).start()
 
-                    o = t - 3
+                    o = t - 4
 
                     @pl.when(both(o >= 0, o < RN // 2))
                     def _():
                         for up in range(2):
                             r_ring(2 * o + up, xr(2 * o + up)).wait_send()
 
-                    @pl.when(both(o >= 0, o < RN))
+                    i = t - 8
+
+                    @pl.when(both(i >= 0, i < RN))
                     def _():
-                        r_cross(o, xr(o)).wait_send()
+                        r_cross(i, xr(i)).wait_send()
 
             for up in range(2):
                 hops = z if up == 0 else 8 - z
@@ -305,13 +304,19 @@
 
         def step(t):
             own_line(t)
+            if op:
+
+                @pl.when(t < 8)
+                def _():
+                    c_source(t, True)
+
             for j in range(4):
 
                 @pl.when(t == 20 + 4 * j)
                 def _():
                     other_line(j)
 
-        loop(5 + RN, step)
+        loop(max(5, 8) + RN, step)
 
     def across(half, op):
         def one(i):
@@ -321,8 +326,6 @@
             r_sib(1 - xl, n, op)
 
         loop(RN // 2, one)
-
-    source_copies(True)
 
     @pl.when(is_root)
     def _():
@@ -449,11 +452,9 @@
             def _():
                 f_rows(SCHED[g - 1] if g else 0, SCHED[g], pass_on)
 
-        if g < 2:
-
-            @pl.when(d == 0)
-            def _():
-                across(g, True)
+        @pl.when(both(d == 0, xl == (1 if g < 2 else 0)))
+        def _():
+            across(g % 2, True)
 
         panels_here(g // 2, g % 2)
         if g == 0:
@@ -541,7 +542,7 @@
     for g in range(4):
         loop(2, lambda i: v_copy(g, i).wait_send())
     d_copies(False)
-    source_copies(False)
+    loop(8, lambda i: c_source(i, False))
 
     @pl.when(d == 0)
     def _():

time: 129 us -> 128 us (level)
  the two profiles are of different devices: /device:TPU:38 before, /device:TPU:0 now
where the time goes in v4:
time: 128 us
  Pallas kernels  126 us (98%)
  local copies, waits for them, and re-layouts  2.02 us (2%)
    pallas_call x1, Pallas kernels, call(): pl.pallas_call(kernel, out_shape=pltpu.VMEM((T * L16, B), F32), in_specs=...  126 us

profile of v4, /device:TPU:0, one launch (start us, length us, event | category | flops | bytes accessed | tf_op | source)
XLA Modules:
  0.0 127.6 jit_solution(17460232374617037467)
XLA Ops:
  0.0 125.6 %panels.1 = f32[8192,128]{1,0:T(8,128)S(1)} custom-call(f32[16384,128]{1,0:T(8,128)} %bitcast.4, f32[1024,4,4,128]{3,2,1,0:T(4,128)} %bitcast.5), custom_call_target="tpu_custom_call" | custom-call | tf_op jit(solution)/shard_map/panels/pallas_call | solution.py:560
  125.6 2.0 %copy.4 = f32[2,1,256,4,1,512]{5,4,3,2,1,0:T(1,128)} copy(f32[2,1,256,4,1,512]{5,4,3,2,1,0:T(1,128)S(1)} %bitcast.3) | data formatting | bytes 8388608
